TPU v7x, 256 devices: a whole 4x4x8 slice. The times are simulated.
256 devices in a mesh: scan: 32 (over z, y), lat: 8 (over x, core).
Axes of the slice: x: 4, y: 4, z: 8, core: 2. Of those that a mesh axis runs over, the one named last changes fastest.
Arguments:
- observed: bfloat16 [384, 512, 512], P('scan', 'lat'), may hold values from 0.099609375 to 4
- estimate: float32 [384, 512, 512], P('scan', 'lat'), may hold values from 0.1 to 4
- column_weights: float32 [512, 512], replicated, may hold values from 0 to 0.5, as said below
- plane_taps: float32 [7], replicated, may hold values from 0.1 to 1
- row_taps: float32 [7], replicated, may hold values from 0.1 to 1
- shear_planes: int32 [512], replicated, may hold values from 1 to 383, as said below
Outputs:
- deskewed: float32 [384, 512, 512], P('scan', 'lat')
Inputs may be any that keep to these rules, and one draw needn't show every extreme that they name: `shear_planes`: never falls from one column to the next; the first column's offset is 1 and the last column's is 383. `column_weights`: zero more than 8 columns away from the diagonal, positive within.
All inputs are finite; a program needn't handle non-finite values.
Results may differ from a plain program's by a relative error of at most 0.0003.
Values sent between devices are 32-bit elements; how exact they have to be, the bound alone decides.
A program may use at most 64 MiB of HBM per device.

v0:
```python
import jax
import jax.numpy as jnp
from jax import lax
from jax.sharding import PartitionSpec as P

PLANE_HALF = 3
ROW_HALF = 3
SKEW = 2


def padded_2(cells, sides, width):
    for axis, dim in sides:
        count = lax.axis_size(axis)
        ends = count - 1
        head = lax.slice_in_dim(cells, 0, width, axis=dim)
        tail = lax.slice_in_dim(cells, cells.shape[dim] - width, cells.shape[dim], axis=dim)
        cells = jnp.concatenate(
            [
                lax.ppermute(tail, axis, [(i, (i + 1) % count) for i in range(ends)]),
                cells,
                lax.ppermute(head, axis, [((i + 1) % count, i) for i in range(ends)]),
            ],
            axis=dim,
        )
    return cells


def column_mix(field, matrix):
    flat = field.reshape(-1, matrix.shape[0])
    mixed = jnp.dot(
        flat, matrix, precision=lax.Precision.HIGHEST, preferred_element_type=jnp.float32
    )
    return mixed.reshape(field.shape)


def row_pass(padded, kernel, direction):
    halfwidth = (kernel.shape[0] - 1) // 2
    row_count = padded.shape[1] - 2 * halfwidth
    summed = jnp.zeros((padded.shape[0], row_count, padded.shape[2]), jnp.float32)
    for offset in range(-halfwidth, halfwidth + 1):
        begin = halfwidth + direction * offset
        summed = summed + kernel[offset + halfwidth] * padded[:, begin : begin + row_count, :]
    return summed


def plane_pass(padded, kernel, direction):
    halfwidth = (kernel.shape[0] - 1) // 2
    plane_count = padded.shape[0] - 2 * halfwidth
    column_count = padded.shape[2]
    widened = jnp.pad(padded, ((0, 0), (0, 0), (halfwidth * SKEW, halfwidth * SKEW)))
    summed = jnp.zeros((plane_count, padded.shape[1], column_count), jnp.float32)
    for offset in range(-halfwidth, halfwidth + 1):
        begin = halfwidth + direction * offset
        column_start = halfwidth * SKEW - direction * offset * SKEW
        summed = (
            summed
            + kernel[offset + halfwidth]
            * widened[begin : begin + plane_count, :, column_start : column_start + column_count]
        )
    return summed


def row_rim(field):
    return padded_2(field, (("lat", 1),), ROW_HALF)


def plane_rim(field):
    return padded_2(field, (("scan", 0),), PLANE_HALF)


def shift_down(field, amount):
    filler = jnp.zeros((amount,) + field.shape[1:], field.dtype)
    return jnp.concatenate([filler, field[: field.shape[0] - amount]], 0)


def shear_columns(field, offsets):
    plane_count = field.shape[0]
    for bit_place in range((plane_count - 1).bit_length()):
        amount = 1 << bit_place
        chosen = (offsets >> bit_place & 1 == 1)[None, None, :]
        moved = shift_down(field, amount)
        field = jnp.where(chosen, moved, field)
    return field


def on_device(observed, estimate, column_weights, plane_taps, row_taps, shear_planes):
    plane_count, row_count, column_count = estimate.shape
    mixed_cols = column_mix(estimate, column_weights)
    row_blur = row_pass(row_rim(mixed_cols), row_taps, 1)
    blurred = plane_pass(plane_rim(row_blur), plane_taps, 1)
    quotient = observed.astype(jnp.float32) / blurred
    back_planes = plane_pass(plane_rim(quotient), plane_taps, -1)
    back_rows = row_pass(row_rim(back_planes), row_taps, -1)
    correction = column_mix(back_rows, column_weights.T)
    updated = estimate * correction
    group_cols = column_count // lax.axis_size("scan")
    own_shear = lax.dynamic_slice_in_dim(
        shear_planes, lax.axis_index("scan") * group_cols, group_cols
    )
    settled = shear_columns(
        lax.all_to_all(updated, "scan", split_axis=2, concat_axis=0, tiled=True), own_shear
    )
    return lax.all_to_all(settled, "scan", split_axis=0, concat_axis=2, tiled=True)


def solution(mesh):
    placed = (P("scan", "lat", None), P("scan", "lat", None), P(), P(), P(), P())
    return jax.shard_map(
        on_device, mesh=mesh, in_specs=placed, out_specs=P("scan", "lat", None), check_vma=False
    )
```

profile of v0, /device:TPU:2, one launch (start us, length us, event | category | flops | bytes accessed | tf_op | source)
XLA Modules:
  0.0 233.4 jit_solution(12738872336963184721)
XLA Ops:
  1.2 4.0 %fusion.60 = f32[12,64,512]{2,1,0:T(8,128)S(1)} fusion(f32[12,64,512]{2,1,0:T(8,128)} %param.7, f32[512,512]{1,0:T(8,128)S(1)} %copy-done), kind=kOutput, calls=%fused_computation.99 | convolution fusion | flops 2415919104 | bytes 4194304 | tf_op jit(solution)/shard_map/dot_general | solution.py:30
  5.3 1.9 collective-permute-start
  7.2 3.6 %collective-permute-start.1 = (f32[12,3,512]{2,1,0:T(4,128)S(1)}, f32[12,3,512]{2,1,0:T(4,128)S(1)}, u32[]{:S(2)}, u32[]{:S(2)}) collective-permute-start(f32[12,3,512]{2,1,0:T(4,128)S(1)} %get-tuple-element.14), channel_id=1, source_target_pairs={{1,0},{2,1},{3,2},{4,3},{5,4},{6,5},{7,6},{9,8},{10,9},{11,10},{12... | collective-permute-start | bytes 221192 | tf_op jit(solution)/shard_map/ppermute | solution.py:21
  11.6 1.5 collective-permute-done.1
  13.1 6.0 %fusion.23 = f32[12,64,512]{2,1,0:T(8,128)S(1)} fusion(f32[12,64,512]{2,1,0:T(8,128)S(1)} %fusion.60, f32[12,3,512]{2,1,0:T(4,128)S(1)} %collective-permute-done.1, f32[12,3,512]{2,1,0:T(4,128)S(1)} %collective-permute-done, f32[]{:T(128)} %bitcast.8, f32[]{:T(128)} %bitcast.7, f32[]{:T(128)} %bitcast.6, f32[]{:T(128)} %bitcast.5, f32[]{:T(128)} %bitcast.4, ...), kind=kLoop, calls=%fused_computation.50 | loop fusion | flops 7471104 | bytes 3293212 | tf_op jit(solution)/shard_map/add | solution.py:42
  19.2 3.5 %collective-permute-start.2 = (f32[3,64,512]{2,1,0:T(8,128)S(1)}, f32[3,64,512]{2,1,0:T(8,128)S(1)}, u32[]{:S(2)}, u32[]{:S(2)}) collective-permute-start(f32[3,64,512]{2,1,0:T(8,128)S(1)} %get-tuple-element.11), channel_id=1, source_target_pairs={{0,8},{8,16},{16,24},{24,32},{32,40},{40,48},{48,56},{56,64},{64,7... | collective-permute-start | bytes 1179656 | tf_op jit(solution)/shard_map/ppermute | solution.py:19
  22.7 1.3 collective-permute-start.3
  24.7 6.8 %collective-permute-done.2 = f32[3,64,512]{2,1,0:T(8,128)S(1)} collective-permute-done((f32[3,64,512]{2,1,0:T(8,128)S(1)}, f32[3,64,512]{2,1,0:T(8,128)S(1)}, u32[]{:S(2)}, u32[]{:S(2)}) %collective-permute-start.2) | collective-permute-done | bytes 393248 | tf_op jit(solution)/shard_map/ppermute | solution.py:19
  31.5 4.7 %collective-permute-done.3 = f32[3,64,512]{2,1,0:T(8,128)S(1)} collective-permute-done((f32[3,64,512]{2,1,0:T(8,128)S(1)}, f32[3,64,512]{2,1,0:T(8,128)S(1)}, u32[]{:S(2)}, u32[]{:S(2)}) %collective-permute-start.3) | collective-permute-done | bytes 393248 | tf_op jit(solution)/shard_map/ppermute | solution.py:21
  37.0 6.6 %fusion.47 = f32[12,64,512]{2,1,0:T(8,128)S(1)} fusion(f32[18,64,524]{2,1,0:T(8,128)S(1)} %select_maximum_fusion.2, f32[12,64,512]{2,1,0:T(8,128)S(1)} %fusion.23, bf16[12,64,512]{2,1,0:T(8,128)(2,1)S(1)} %copy-done.3, f32[]{:T(128)} %bitcast.14, f32[]{:T(128)} %bitcast.13, f32[]{:T(128)} %bitcast.12, f32[]{:T(128)} %bitcast.11, f32[]{:T(128)} %bitcast.10, ...), kind=kLoop, calls=%fused_computation.81 | loop fusion | flops 5898240 | bytes 13369372 | tf_op jit(solution)/shard_map/div | solution.py:91
  43.7 3.5 %collective-permute-start.4 = (f32[3,64,512]{2,1,0:T(8,128)S(1)}, f32[3,64,512]{2,1,0:T(8,128)S(1)}, u32[]{:S(2)}, u32[]{:S(2)}) collective-permute-start(f32[3,64,512]{2,1,0:T(8,128)S(1)} %get-tuple-element.9), channel_id=1, source_target_pairs={{0,8},{8,16},{16,24},{24,32},{32,40},{40,48},{48,56},{56,64},{64,7... | collective-permute-start | bytes 1179656 | tf_op jit(solution)/shard_map/ppermute | solution.py:19
  48.5 7.5 %collective-permute-done.4 = f32[3,64,512]{2,1,0:T(8,128)S(1)} collective-permute-done((f32[3,64,512]{2,1,0:T(8,128)S(1)}, f32[3,64,512]{2,1,0:T(8,128)S(1)}, u32[]{:S(2)}, u32[]{:S(2)}) %collective-permute-start.4) | collective-permute-done | bytes 393248 | tf_op jit(solution)/shard_map/ppermute | solution.py:19
  55.9 4.1 %collective-permute-done.5 = f32[3,64,512]{2,1,0:T(8,128)S(1)} collective-permute-done((f32[3,64,512]{2,1,0:T(8,128)S(1)}, f32[3,64,512]{2,1,0:T(8,128)S(1)}, u32[]{:S(2)}, u32[]{:S(2)}) %collective-permute-start.5) | collective-permute-done | bytes 393248 | tf_op jit(solution)/shard_map/ppermute | solution.py:21
  60.9 6.7 %fusion.40 = f32[12,64,512]{2,1,0:T(8,128)S(1)} fusion(f32[18,64,524]{2,1,0:T(8,128)S(1)} %select_maximum_fusion, f32[12,64,512]{2,1,0:T(8,128)S(1)} %fusion.47, f32[]{:T(128)} %bitcast.14, f32[]{:T(128)} %bitcast.13, f32[]{:T(128)} %bitcast.12, f32[]{:T(128)} %bitcast.11, f32[]{:T(128)} %bitcast.10, f32[]{:T(128)} %bitcast.9, f32[]{:T(128)} %bitcast.1), kind=kLoop, calls=%fused_computation.68 | loop fusion | flops 5111808 | bytes 12582940 | tf_op jit(solution)/shard_map/add | solution.py:56
  67.6 1.9 collective-permute-start.6
  69.6 2.6 %collective-permute-start.7 = (f32[12,3,512]{2,1,0:T(4,128)S(1)}, f32[12,3,512]{2,1,0:T(4,128)S(1)}, u32[]{:S(2)}, u32[]{:S(2)}) collective-permute-start(f32[12,3,512]{2,1,0:T(4,128)S(1)} %get-tuple-element.8), channel_id=1, source_target_pairs={{0,1},{1,2},{2,3},{3,4},{4,5},{5,6},{6,7},{8,9},{9,10},{10,11},{11... | collective-permute-start | bytes 221192 | tf_op jit(solution)/shard_map/ppermute | solution.py:19
  72.2 3.3 %collective-permute-done.7 = f32[12,3,512]{2,1,0:T(4,128)S(1)} collective-permute-done((f32[12,3,512]{2,1,0:T(4,128)S(1)}, f32[12,3,512]{2,1,0:T(4,128)S(1)}, u32[]{:S(2)}, u32[]{:S(2)}) %collective-permute-start.7) | collective-permute-done | bytes 73760 | tf_op jit(solution)/shard_map/ppermute | solution.py:19
  75.5 8.4 %fusion.56 = f32[12,64,512]{2,1,0:T(8,128)S(1)} fusion(f32[12,64,512]{2,1,0:T(8,128)S(1)} %copy-done.2, f32[12,64,512]{2,1,0:T(8,128)S(1)} %fusion.40, f32[12,3,512]{2,1,0:T(4,128)S(1)} %collective-permute-done.7, f32[12,3,512]{2,1,0:T(4,128)S(1)} %collective-permute-done.6, f32[512,512]{1,0:T(8,128)S(1)} %copy-done, f32[]{:T(128)} %bitcast.8, f32[]{:T(128)} %bitcast.7, ...), kind=kOutput, calls=%fused_computation.97 | convolution fusion | flops 2423783424 | bytes 5914652 | tf_op jit(solution)/shard_map/dot_general | solution.py:30
  83.9 3.7 %copy.11 = f32[12,64,512]{1,0,2:T(8,128)} copy(f32[12,64,512]{2,1,0:T(8,128)S(1)} %fusion.56) | data formatting | bytes 3145728 | tf_op jit(solution)/shard_map/mul | solution.py:95
  87.7 5.0 %reshape.18 = f32[32,1,12288]{2,1,0:T(1,128)} reshape(f32[512,12,64]{2,1,0:T(8,128)} %bitcast.36) | data formatting | bytes 3145728
  92.7 15.3 %all-to-all-start = ((f32[32,1,12288]{2,1,0:T(1,128)}), f32[32,1,12288]{2,1,0:T(1,128)S(1)}, u32[]{:S(2)}, u32[]{:S(2)}) async-start(f32[32,1,12288]{2,1,0:T(1,128)} %reshape.18), calls=%async_computation | async-start | bytes 3145728 | tf_op jit(solution)/shard_map/all_to_all | solution.py:101
  108.8 37.8 %all-to-all-done = f32[32,1,12288]{2,1,0:T(1,128)S(1)} async-done(((f32[32,1,12288]{2,1,0:T(1,128)}), f32[32,1,12288]{2,1,0:T(1,128)S(1)}, u32[]{:S(2)}, u32[]{:S(2)}) %all-to-all-start) | async-done | bytes 1572896 | tf_op jit(solution)/shard_map/all_to_all | solution.py:101
  147.1 6.0 %reduce = f32[32,12288]{1,0:T(8,128)} reduce(f32[32,1,12288]{2,1,0:T(1,128)S(1)} %all-to-all-done, f32[]{:T(128)} %broadcast.108), dimensions={1}, to_apply=%all_to_all.26.reduce_sub_computation | reduce | bytes 3145732 | tf_op jit(solution)/shard_map/all_to_all | solution.py:101
  153.1 3.7 %reshape.19 = f32[512,12,64]{2,1,0:T(8,128)} reshape(f32[32,12288]{1,0:T(8,128)} %reduce) | data formatting | bytes 3145728
  156.8 3.5 %copy.13 = f32[32,12,64,16]{2,3,1,0:T(8,128)S(1)} copy(f32[32,12,64,16]{2,1,3,0:T(8,128)} %bitcast.35) | data formatting | bytes 3145728 | tf_op jit(solution)/shard_map/all_to_all | solution.py:101
  165.4 2.0 fusion.76
  167.4 4.4 %reshape.20 = f32[32,1,12288]{2,1,0:T(1,128)} reshape(f32[384,16,64]{2,1,0:T(8,128)} %fusion.76) | data formatting | bytes 3145728
  171.8 44.9 %all_to_all.36 = f32[32,1,12288]{2,1,0:T(1,128)S(1)} all-to-all(f32[32,1,12288]{2,1,0:T(1,128)} %reshape.20), channel_id=1, replica_groups=mesh['scan'=32,'lat'=8] {'scan'}, dimensions={0} | all-to-all | bytes 3145728 | tf_op jit(solution)/shard_map/all_to_all | solution.py:103
  216.7 6.0 %reduce.1 = f32[32,12288]{1,0:T(8,128)} reduce(f32[32,1,12288]{2,1,0:T(1,128)S(1)} %all_to_all.36, f32[]{:T(128)} %broadcast.108), dimensions={1}, to_apply=%all_to_all.30.reduce_sub_computation | reduce | bytes 3145732 | tf_op jit(solution)/shard_map/all_to_all | solution.py:103
  222.7 3.5 %reshape.21 = f32[384,16,64]{2,1,0:T(8,128)} reshape(f32[32,12288]{1,0:T(8,128)} %reduce.1) | data formatting | bytes 3145728
  226.2 3.9 %copy.14 = f32[12,64,32,16]{1,3,2,0:T(8,128)} copy(f32[12,64,32,16]{1,3,0,2:T(8,128)} %bitcast.37) | data formatting | bytes 3145728 | tf_op jit(solution)/shard_map/all_to_all | solution.py:103
  230.1 3.3 %copy.15 = f32[12,64,512]{2,1,0:T(8,128)} copy(f32[12,64,512]{1,2,0:T(8,128)} %bitcast.38) | data formatting | bytes 3145728 | tf_op jit(solution)/shard_map/all_to_all | solution.py:103
  (43 shorter events, 12.1 us)
Async XLA Ops:
  0.0 1.2 copy-start
  0.0 10.9 %copy-start.4 = (f32[7]{0:T(128)S(1)}, f32[7]{0:T(128)}, u32[]{:S(2)}) copy-start(f32[7]{0:T(128)} %param.10) | copy-start | bytes 88
  5.3 6.3 %collective-permute-start = (f32[12,3,512]{2,1,0:T(4,128)S(1)}, f32[12,3,512]{2,1,0:T(4,128)S(1)}, u32[]{:S(2)}, u32[]{:S(2)}) collective-permute-start(f32[12,3,512]{2,1,0:T(4,128)S(1)} %get-tuple-element.13), channel_id=1, source_target_pairs={{0,1},{1,2},{2,3},{3,4},{4,5},{5,6},{6,7},{8,9},{9,10},{10,11},{11... | collective-permute-start | bytes 221192 | tf_op jit(solution)/shard_map/ppermute | solution.py:19
  7.2 5.8 %collective-permute-start.1 = (f32[12,3,512]{2,1,0:T(4,128)S(1)}, f32[12,3,512]{2,1,0:T(4,128)S(1)}, u32[]{:S(2)}, u32[]{:S(2)}) collective-permute-start(f32[12,3,512]{2,1,0:T(4,128)S(1)} %get-tuple-element.14), channel_id=1, source_target_pairs={{1,0},{2,1},{3,2},{4,3},{5,4},{6,5},{7,6},{9,8},{10,9},{11,10},{12... | collective-permute-start | bytes 221192 | tf_op jit(solution)/shard_map/ppermute | solution.py:21
  19.1 4.9 %copy-start.5 = (f32[7]{0:T(128)S(1)}, f32[7]{0:T(128)}, u32[]{:S(2)}) copy-start(f32[7]{0:T(128)} %param.9) | copy-start | bytes 88
  19.2 12.3 %collective-permute-start.2 = (f32[3,64,512]{2,1,0:T(8,128)S(1)}, f32[3,64,512]{2,1,0:T(8,128)S(1)}, u32[]{:S(2)}, u32[]{:S(2)}) collective-permute-start(f32[3,64,512]{2,1,0:T(8,128)S(1)} %get-tuple-element.11), channel_id=1, source_target_pairs={{0,8},{8,16},{16,24},{24,32},{32,40},{40,48},{48,56},{56,64},{64,7... | collective-permute-start | bytes 1179656 | tf_op jit(solution)/shard_map/ppermute | solution.py:19
  22.7 13.4 %collective-permute-start.3 = (f32[3,64,512]{2,1,0:T(8,128)S(1)}, f32[3,64,512]{2,1,0:T(8,128)S(1)}, u32[]{:S(2)}, u32[]{:S(2)}) collective-permute-start(f32[3,64,512]{2,1,0:T(8,128)S(1)} %get-tuple-element.12), channel_id=1, source_target_pairs={{8,0},{16,8},{24,16},{32,24},{40,32},{48,40},{56,48},{64,56},{72,6... | collective-permute-start | bytes 1179656 | tf_op jit(solution)/shard_map/ppermute | solution.py:21
  24.7 12.3 %copy-start.3 = (bf16[12,64,512]{2,1,0:T(8,128)(2,1)S(1)}, bf16[12,64,512]{2,1,0:T(8,128)(2,1)}, u32[]{:S(2)}) copy-start(bf16[12,64,512]{2,1,0:T(8,128)(2,1)} %param.6) | copy-start | bytes 2359300
  43.7 12.2 %collective-permute-start.4 = (f32[3,64,512]{2,1,0:T(8,128)S(1)}, f32[3,64,512]{2,1,0:T(8,128)S(1)}, u32[]{:S(2)}, u32[]{:S(2)}) collective-permute-start(f32[3,64,512]{2,1,0:T(8,128)S(1)} %get-tuple-element.9), channel_id=1, source_target_pairs={{0,8},{8,16},{16,24},{24,32},{32,40},{40,48},{48,56},{56,64},{64,7... | collective-permute-start | bytes 1179656 | tf_op jit(solution)/shard_map/ppermute | solution.py:19
  47.2 12.9 %collective-permute-start.5 = (f32[3,64,512]{2,1,0:T(8,128)S(1)}, f32[3,64,512]{2,1,0:T(8,128)S(1)}, u32[]{:S(2)}, u32[]{:S(2)}) collective-permute-start(f32[3,64,512]{2,1,0:T(8,128)S(1)} %get-tuple-element.10), channel_id=1, source_target_pairs={{8,0},{16,8},{24,16},{32,24},{40,32},{48,40},{56,48},{64,56},{72,6... | collective-permute-start | bytes 1179656 | tf_op jit(solution)/shard_map/ppermute | solution.py:21
  60.9 14.6 %copy-start.2 = (f32[12,64,512]{2,1,0:T(8,128)S(1)}, f32[12,64,512]{2,1,0:T(8,128)}, u32[]{:S(2)}) copy-start(f32[12,64,512]{2,1,0:T(8,128)} %param.7) | copy-start | bytes 4718596
  67.6 4.5 %collective-permute-start.6 = (f32[12,3,512]{2,1,0:T(4,128)S(1)}, f32[12,3,512]{2,1,0:T(4,128)S(1)}, u32[]{:S(2)}, u32[]{:S(2)}) collective-permute-start(f32[12,3,512]{2,1,0:T(4,128)S(1)} %get-tuple-element.7), channel_id=1, source_target_pairs={{1,0},{2,1},{3,2},{4,3},{5,4},{6,5},{7,6},{9,8},{10,9},{11,10},{12... | collective-permute-start | bytes 221192 | tf_op jit(solution)/shard_map/ppermute | solution.py:21
  69.6 5.9 %collective-permute-start.7 = (f32[12,3,512]{2,1,0:T(4,128)S(1)}, f32[12,3,512]{2,1,0:T(4,128)S(1)}, u32[]{:S(2)}, u32[]{:S(2)}) collective-permute-start(f32[12,3,512]{2,1,0:T(4,128)S(1)} %get-tuple-element.8), channel_id=1, source_target_pairs={{0,1},{1,2},{2,3},{3,4},{4,5},{5,6},{6,7},{8,9},{9,10},{10,11},{11... | collective-permute-start | bytes 221192 | tf_op jit(solution)/shard_map/ppermute | solution.py:19
  92.7 53.9 %all-to-all-start = ((f32[32,1,12288]{2,1,0:T(1,128)}), f32[32,1,12288]{2,1,0:T(1,128)S(1)}, u32[]{:S(2)}, u32[]{:S(2)}) async-start(f32[32,1,12288]{2,1,0:T(1,128)} %reshape.18), calls=%async_computation | async-start | bytes 3145728 | tf_op jit(solution)/shard_map/all_to_all | solution.py:101
  230.1 3.3 %copy-start.1 = (f32[512,512]{1,0:T(8,128)S(1)}, f32[512,512]{1,0:T(8,128)}, u32[]{:S(2)}) copy-start(f32[512,512]{1,0:T(8,128)} %param.8) | copy-start | bytes 3145732
where the time goes:
time: 234 us; the launch traced here: 233 us
  waiting for transfers between devices  65.7 us (28%)
  blocking collectives  44.9 us (19%)
  other arithmetic  39 us (17%)
  local copies, waits for them, and re-layouts  36.1 us (15%)
  starting transfers between devices  34.9 us (15%)
  matrix products  12.5 us (5%)
    all_to_all x1, blocking collectives, on_device(): lax.all_to_all(settled, 'scan', split_axis=0, concat_axis=2, tiled=True)  44.9 us
    all_to_all x1, waiting for transfers between devices, on_device(): lax.all_to_all(updated, 'scan', split_axis=2, concat_axis=0, tiled=True)  37.8 us
    unnamed x16, local copies, waits for them, and re-layouts  18 us
    ppermute x4, waiting for transfers between devices, padded_2(): lax.ppermute(tail, axis, [(i, (i + 1) % count) for i in range(ends)])  17.5 us
    all_to_all x1, starting transfers between devices, on_device(): lax.all_to_all(updated, 'scan', split_axis=2, concat_axis=0, tiled=True)  15.3 us
    dot_general x2, matrix products, column_mix(): jnp.dot(flat, matrix, precision=lax.Precision.HIGHEST, preferred_element_...  12.5 us
    ppermute x4, starting transfers between devices, padded_2(): lax.ppermute(tail, axis, [(i, (i + 1) % count) for i in range(ends)])  11.5 us
    ppermute x4, waiting for transfers between devices, padded_2(): lax.ppermute(head, axis, [((i + 1) % count, i) for i in range(ends)])  10.3 us
  transfers between devices with their start and end apart: 9, of which 7 were waited for; matrix products, arithmetic and copies ran while one was open for 1% of the time, Pallas kernels for 0%

commit v1 on v0

v1 whole, which is shorter than its diff:
```python
import functools

import jax
import jax.numpy as jnp
from jax import lax
from jax.experimental import pallas as pl
from jax.experimental.pallas import tpu as pltpu
from jax.sharding import PartitionSpec as P

MESH = pl.DeviceIdType.MESH
F32 = jnp.float32
BF16 = jnp.bfloat16
PLANES = 12
PAIRS = 6
ROWS = 64
COLS = 512
LANES = 128
TILES = COLS // LANES
PAD = 8


def split(x):
    hi = x.astype(BF16)
    return hi, (x - hi.astype(F32)).astype(BF16)


def dot(a, b):
    return jnp.dot(a, b, preferred_element_type=F32)


def lane_ids(rows):
    return lax.broadcasted_iota(jnp.int32, (rows, LANES), 1)


def half_roll(x):
    return pltpu.roll(x, ROWS, 1)


def row_matrix(taps, flip):
    line = lax.broadcasted_iota(jnp.int32, (LANES, LANES), 0)
    column = lax.broadcasted_iota(jnp.int32, (LANES, LANES), 1)
    same = (line >= ROWS) == (column >= ROWS)
    row = line & (ROWS - 1)
    target = column & (ROWS - 1)
    far = jnp.where(row < ROWS // 2, row + ROWS, row - ROWS)
    own = jnp.zeros((LANES, LANES), F32)
    edge = jnp.zeros((LANES, LANES), F32)
    for b in range(-3, 4):
        tap = taps[3 - b] if flip else taps[b + 3]
        own = jnp.where(same & (row - target == b), tap, own)
        edge = jnp.where(same & (far - target == b), tap, edge)
    return jnp.concatenate([own, edge], axis=0)


def kernel(
    n,
    nl,
    obs_h,
    est_h,
    w_h,
    pt,
    rt,
    sh,
    out_h,
    obs,
    est,
    w,
    est_t,
    obs_t,
    wmat,
    tmat,
    edge_s,
    edge_r,
    rim_s,
    rim_r,
    hc,
    zf,
    bp,
    rhi,
    rlo,
    upd,
    got,
    lined,
    back,
    fin,
    outv,
    in_sem,
    edge_ss,
    edge_rs,
    rim_ss,
    rim_rs,
    a_ss,
    a_rs,
    b_ss,
    b_rs,
    own_sem,
):
    group = COLS // n
    pitch = 2 * PLANES * n + 9
    me = lax.axis_index("scan")
    lat = lax.axis_index("lat")
    s_prev, s_next = lax.rem(me + n - 1, n), lax.rem(me + 1, n)
    l_prev, l_next = lax.rem(lat + nl - 1, nl), lax.rem(lat + 1, nl)

    barrier = pltpu.get_barrier_semaphore()

    def greet(k, carry):
        pl.semaphore_signal(barrier, inc=1, device_id={"scan": lax.rem(me + k, n), "lat": lat}, device_id_type=MESH)
        return carry

    for other in (l_prev, l_next):
        pl.semaphore_signal(barrier, inc=1, device_id={"scan": me, "lat": other}, device_id_type=MESH)
    lax.fori_loop(1, n, greet, 0)

    loads = [
        pltpu.make_async_copy(est_h, est, in_sem.at[0]),
        pltpu.make_async_copy(w_h, w, in_sem.at[1]),
        pltpu.make_async_copy(obs_h, obs, in_sem.at[2]),
    ]
    for load in loads:
        load.start()

    def send_edges(stage, field):
        def chunk(i, carry):
            at = pl.ds(pl.multiple_of(i * 64, 64), 64)
            lane = lane_ids(64)
            packed = jnp.zeros((64, LANES), F32)
            for m in range(PAIRS):
                x = field[m, at, :]
                moved = pltpu.roll(x, 6 * m, 1) if m else x
                window = (lane + (3 + ROWS - 6 * m)) & (ROWS - 1)
                packed = jnp.where(window < 6, moved, packed)
            edge_s[stage, at, :] = packed
            return carry

        lax.fori_loop(0, COLS // 64, chunk, 0)

    def edge_copies(stage):
        return [
            pltpu.make_async_remote_copy(
                src_ref=edge_s.at[stage],
                dst_ref=edge_r.at[stage, i],
                send_sem=edge_ss.at[stage, i],
                recv_sem=edge_rs.at[stage, i],
                device_id={"scan": me, "lat": other},
                device_id_type=MESH,
            )
            for i, other in ((0, l_next), (1, l_prev))
        ]

    def join_edges(stage):
        def chunk(i, carry):
            at = pl.ds(pl.multiple_of(i * 64, 64), 64)
            spot = (lane_ids(64) + 3) & (ROWS - 1)
            first = lax.rem(spot, 6) < 3
            before = jnp.where(lat > 0, edge_r[stage, 0, at, :], 0.0)
            after = jnp.where(lat < nl - 1, edge_r[stage, 1, at, :], 0.0)
            hc[at, :] = jnp.where(first, before, after)
            return carry

        lax.fori_loop(0, COLS // 64, chunk, 0)

    def row_pass(stage, field):
        def chunk(i, carry):
            at = pl.ds(pl.multiple_of(i * LANES, LANES), LANES)
            edges = hc[at, :]
            for m in range(PAIRS):
                moved = pltpu.roll(edges, LANES - 6 * m, 1) if m else edges
                hi, lo = split(jnp.concatenate([field[m, at, :], moved], axis=1))
                t_hi, t_lo = tmat[stage, 0], tmat[stage, 1]
                y_hi, y_lo = split(dot(hi, t_hi) + dot(lo, t_hi) + dot(hi, t_lo))
                rhi[at, m * LANES : (m + 1) * LANES] = y_hi
                rlo[at, m * LANES : (m + 1) * LANES] = y_lo
            return carry

        lax.fori_loop(0, TILES, chunk, 0)

    def mix(stage, store):
        for b in range(TILES):
            k0, k1 = max(0, b - 1) * LANES, min(TILES, b + 2) * LANES
            block = slice(b * LANES, (b + 1) * LANES)
            w_hi, w_lo = wmat[stage, 0, block, k0:k1], wmat[stage, 1, block, k0:k1]
            for pair in range(PAIRS // 2):
                lanes = slice(pair * 2 * LANES, (pair + 1) * 2 * LANES)
                x_hi, x_lo = rhi[k0:k1, lanes], rlo[k0:k1, lanes]
                y = dot(w_hi, x_hi) + dot(w_hi, x_lo) + dot(w_lo, x_hi)
                store(2 * pair, b, y[:, :LANES])
                store(2 * pair + 1, b, y[:, LANES:])

    def pack_rims(stage):
        def chunk(i, carry):
            lane = lane_ids(64)
            low = lane < ROWS
            r = pl.multiple_of(i * 64, 64)
            at = pl.ds(r + PAD, 64)
            rim_s[stage, 0, pl.ds(r, 64), :] = jnp.where(low, half_roll(zf[6, at, :]), zf[7, at, :])
            rim_s[stage, 1, pl.ds(r, 64), :] = jnp.where(low, zf[3, at, :], half_roll(zf[4, at, :]))
            return carry

        lax.fori_loop(0, COLS // 64, chunk, 0)

        def rest(i, carry):
            low = lane_ids(64) < ROWS
            r = pl.multiple_of(i * 64, 64)
            at, far = pl.ds(r + PAD, 64), pl.ds(r + PAD + COLS // 2, 64)
            rim_s[stage, 0, pl.ds(r + COLS, 64), :] = jnp.where(low, half_roll(zf[8, at, :]), zf[8, far, :])
            rim_s[stage, 1, pl.ds(r + COLS, 64), :] = jnp.where(low, zf[5, at, :], half_roll(zf[5, far, :]))
            return carry

        lax.fori_loop(0, COLS // 128, rest, 0)

    def rim_copies(stage):
        return [
            pltpu.make_async_remote_copy(
                src_ref=rim_s.at[stage, i],
                dst_ref=rim_r.at[stage, i],
                send_sem=rim_ss.at[stage, i],
                recv_sem=rim_rs.at[stage, i],
                device_id={"scan": other, "lat": lat},
                device_id_type=MESH,
            )
            for i, other in ((0, s_next), (1, s_prev))
        ]

    def unpack_rims(stage):
        def chunk(i, carry):
            low = lane_ids(64) < ROWS
            r = pl.multiple_of(i * 64, 64)
            at = pl.ds(r + PAD, 64)
            before = jnp.where(me > 0, rim_r[stage, 0, pl.ds(r, 64), :], 0.0)
            after = jnp.where(me < n - 1, rim_r[stage, 1, pl.ds(r, 64), :], 0.0)
            zf[0, at, :] = jnp.where(low, before, half_roll(zf[6, at, :]))
            zf[1, at, :] = half_roll(jnp.where(low, zf[7, at, :], before))
            zf[9, at, :] = half_roll(jnp.where(low, after, zf[3, at, :]))
            zf[10, at, :] = jnp.where(low, half_roll(zf[4, at, :]), after)
            return carry

        lax.fori_loop(0, COLS // 64, chunk, 0)

        def rest(i, carry):
            low = lane_ids(64) < ROWS
            r = pl.multiple_of(i * 64, 64)
            at, far = pl.ds(r + PAD, 64), pl.ds(r + PAD + COLS // 2, 64)
            before = jnp.where(me > 0, rim_r[stage, 0, pl.ds(r + COLS, 64), :], 0.0)
            after = jnp.where(me < n - 1, rim_r[stage, 1, pl.ds(r + COLS, 64), :], 0.0)
            zf[2, at, :] = jnp.where(low, before, half_roll(zf[8, at, :]))
            zf[2, far, :] = half_roll(jnp.where(low, zf[8, far, :], before))
            zf[11, at, :] = half_roll(jnp.where(low, after, zf[5, at, :]))
            zf[11, far, :] = jnp.where(low, half_roll(zf[5, far, :]), after)
            return carry

        lax.fori_loop(0, COLS // 128, rest, 0)

    def plane_pass(flip, store):
        taps = [pt[3 - a] if flip else pt[a + 3] for a in range(-3, 4)]

        def chunk(i, carry):
            r = pl.multiple_of(i * 64, 64)
            for m in range(PAIRS):
                total = None
                for a in range(-3, 4):
                    term = taps[a + 3] * zf[m + 3 + a, pl.ds(r + (PAD - 2 * a), 64), :]
                    total = term if total is None else total + term
                store(m, r, total)
            return carry

        lax.fori_loop(0, COLS // 64, chunk, 0)

    for m in range(2 * PAIRS):
        zf[m, 0:PAD, :] = jnp.zeros((PAD, LANES), F32)
        zf[m, PAD + COLS : PAD + COLS + PAD, :] = jnp.zeros((PAD, LANES), F32)

    def clear(i, carry):
        for c in range(group):
            lined[pl.ds(c * pitch + 8 * i, 8), :] = jnp.zeros((8, LANES), F32)
        return carry

    loads[0].wait()

    def turn(source, target):
        def one(m, carry):
            for k in range(TILES):
                lanes = slice(k * LANES, (k + 1) * LANES)
                x = jnp.concatenate([source[m, :, lanes], source[m + PAIRS, :, lanes]], axis=0)
                target[m, lanes, :] = x.astype(F32).T
            return carry

        lax.fori_loop(0, PAIRS, one, 0)

    turn(est, est_t)
    send_edges(0, est_t)
    pl.semaphore_wait(barrier, n + 1)
    edges = edge_copies(0)
    for copy in edges:
        copy.start()

    lax.fori_loop(0, PLANES * n // 8, clear, 0)
    for stage in range(2):
        hi, lo = split(row_matrix(rt, stage == 1))
        tmat[stage, 0] = hi
        tmat[stage, 1] = lo
    loads[1].wait()
    for i in range(TILES):
        for j in range(TILES):
            x = w[i * LANES : (i + 1) * LANES, j * LANES : (j + 1) * LANES]
            hi, lo = split(x)
            wmat[1, 0, i * LANES : (i + 1) * LANES, j * LANES : (j + 1) * LANES] = hi
            wmat[1, 1, i * LANES : (i + 1) * LANES, j * LANES : (j + 1) * LANES] = lo
            hi, lo = split(x.T)
            wmat[0, 0, j * LANES : (j + 1) * LANES, i * LANES : (i + 1) * LANES] = hi
            wmat[0, 1, j * LANES : (j + 1) * LANES, i * LANES : (i + 1) * LANES] = lo

    for copy in edges:
        copy.wait()
    join_edges(0)
    row_pass(0, est_t)

    def to_field(m, b, y):
        zf[m + 3, PAD + b * LANES : PAD + (b + 1) * LANES, :] = y

    mix(0, to_field)
    pack_rims(0)
    rims = rim_copies(0)
    for copy in rims:
        copy.start()
    loads[2].wait()
    turn(obs, obs_t)
    for copy in rims:
        copy.wait()
    unpack_rims(0)

    def to_quotient(m, r, total):
        bp[m, pl.ds(r, 64), :] = obs_t[m, pl.ds(r, 64), :] / total

    plane_pass(False, to_quotient)

    def place(i, carry):
        r = pl.multiple_of(i * 64, 64)
        for m in range(PAIRS):
            zf[m + 3, pl.ds(r + PAD, 64), :] = bp[m, pl.ds(r, 64), :]
        return carry

    lax.fori_loop(0, COLS // 64, place, 0)

    pack_rims(1)
    rims = rim_copies(1)
    for copy in rims:
        copy.start()
    for copy in rims:
        copy.wait()
    unpack_rims(1)

    def to_back(m, r, total):
        bp[m, pl.ds(r, 64), :] = total

    plane_pass(True, to_back)
    send_edges(1, bp)
    edges = edge_copies(1)
    for copy in edges:
        copy.start()
    for copy in edges:
        copy.wait()
    join_edges(1)
    row_pass(1, bp)

    def to_updated(m, b, y):
        block = slice(b * LANES, (b + 1) * LANES)
        upd[m, block, :] = est_t[m, block, :] * y

    mix(1, to_updated)

    def first_copy(k):
        dest = lax.rem(me + k, n)
        return pltpu.make_async_remote_copy(
            src_ref=upd.at[:, pl.ds(pl.multiple_of(dest * group, group), group), :],
            dst_ref=got.at[me],
            send_sem=a_ss.at[k],
            recv_sem=a_rs.at[me],
            device_id={"scan": dest, "lat": lat},
            device_id_type=MESH,
        )

    def second_copy(k):
        dest = lax.rem(me + k, n)
        return pltpu.make_async_remote_copy(
            src_ref=back.at[pl.ds(pl.multiple_of(dest * PAIRS * group, 8), PAIRS * group), :],
            dst_ref=fin.at[me],
            send_sem=b_ss.at[k],
            recv_sem=b_rs.at[me],
            device_id={"scan": dest, "lat": lat},
            device_id_type=MESH,
        )

    def start_first(k, carry):
        first_copy(k).start()
        return carry

    lax.fori_loop(1, n, start_first, 0)
    mine = pltpu.make_async_copy(
        upd.at[:, pl.ds(pl.multiple_of(me * group, group), group), :], got.at[me], own_sem.at[0]
    )
    mine.start()
    mine.wait()

    def line_up(s):
        low = lane_ids(8) < ROWS
        for m in range(PAIRS):
            for g in range(group // 8):
                x = got[s, m, 8 * g : 8 * g + 8, :]
                y = half_roll(x)
                start = 8 * g * pitch + PLANES * n + PLANES * s + m
                lined[pl.ds(start, 8, stride=pitch), :] = jnp.where(low, x, y)
                lined[pl.ds(start + PAIRS, 8, stride=pitch), :] = jnp.where(low, y, x)

    line_up(me)

    def take_first(k, carry):
        s = lax.rem(me - k + n, n)
        pltpu.make_async_remote_copy(
            src_ref=upd.at[:, pl.ds(0, group), :],
            dst_ref=got.at[s],
            send_sem=a_ss.at[k],
            recv_sem=a_rs.at[s],
            device_id={"scan": s, "lat": lat},
            device_id_type=MESH,
        ).wait_recv()
        line_up(s)
        return carry

    lax.fori_loop(1, n, take_first, 0)

    def shear(dest):
        low = lane_ids(8) < ROWS
        for c in range(group):
            at = c * pitch + PLANES * n + PLANES * dest - sh[me * group + c]
            x = jnp.where(low, lined[pl.ds(at, 8), :], lined[pl.ds(at + PAIRS, 8), :])
            back[pl.ds(dest * (PAIRS * group) + c, PAIRS, stride=group), :] = x[:PAIRS]

    def start_second(k, carry):
        shear(lax.rem(me + k, n))
        second_copy(k).start()
        return carry

    lax.fori_loop(1, n, start_second, 0)
    shear(me)
    mine = pltpu.make_async_copy(
        back.at[pl.ds(pl.multiple_of(me * PAIRS * group, 8), PAIRS * group), :], fin.at[me], own_sem.at[1]
    )
    mine.start()
    mine.wait()

    def take_second(k, carry):
        s = lax.rem(me - k + n, n)
        pltpu.make_async_remote_copy(
            src_ref=back.at[pl.ds(0, PAIRS * group), :],
            dst_ref=fin.at[s],
            send_sem=b_ss.at[k],
            recv_sem=b_rs.at[s],
            device_id={"scan": s, "lat": lat},
            device_id_type=MESH,
        ).wait_recv()
        return carry

    lax.fori_loop(1, n, take_second, 0)
    per = LANES // group
    for k in range(TILES):
        for m in range(PAIRS):
            x = jnp.concatenate(
                [fin[k * per + j, m * group : (m + 1) * group, :] for j in range(per)], axis=0
            ).T
            outv[m, :, k * LANES : (k + 1) * LANES] = x[:ROWS]
            outv[m + PAIRS, :, k * LANES : (k + 1) * LANES] = x[ROWS:]
    done = pltpu.make_async_copy(outv, out_h, own_sem.at[2])
    done.start()

    def drain(k, carry):
        first_copy(k).wait_send()
        second_copy(k).wait_send()
        return carry

    lax.fori_loop(1, n, drain, 0)
    done.wait()


def solution(mesh):
    n, nl = mesh.shape["scan"], mesh.shape["lat"]
    group = COLS // n
    pitch = 2 * PLANES * n + 9

    def on_device(observed, estimate, column_weights, plane_taps, row_taps, shear_planes):
        any_space = pl.BlockSpec(memory_space=pl.ANY)
        scalars = pl.BlockSpec(memory_space=pltpu.SMEM)
        return pl.pallas_call(
            functools.partial(kernel, n, nl),
            out_shape=jax.ShapeDtypeStruct((PLANES, ROWS, COLS), F32),
            in_specs=[any_space, any_space, any_space, scalars, scalars, scalars],
            out_specs=any_space,
            scratch_shapes=[
                pltpu.VMEM((PLANES, ROWS, COLS), BF16),
                pltpu.VMEM((PLANES, ROWS, COLS), F32),
                pltpu.VMEM((COLS, COLS), F32),
                pltpu.VMEM((PAIRS, COLS, LANES), F32),
                pltpu.VMEM((PAIRS, COLS, LANES), F32),
                pltpu.VMEM((2, 2, COLS, COLS), BF16),
                pltpu.VMEM((2, 2, 2 * LANES, LANES), BF16),
                pltpu.VMEM((2, COLS, LANES), F32),
                pltpu.VMEM((2, 2, COLS, LANES), F32),
                pltpu.VMEM((2, 2, 3 * COLS // 2, LANES), F32),
                pltpu.VMEM((2, 2, 3 * COLS // 2, LANES), F32),
                pltpu.VMEM((COLS, LANES), F32),
                pltpu.VMEM((2 * PAIRS, COLS + 2 * PAD, LANES), F32),
                pltpu.VMEM((PAIRS, COLS, LANES), F32),
                pltpu.VMEM((COLS, PAIRS * LANES), BF16),
                pltpu.VMEM((COLS, PAIRS * LANES), BF16),
                pltpu.VMEM((PAIRS, COLS, LANES), F32),
                pltpu.VMEM((n, PAIRS, group, LANES), F32),
                pltpu.VMEM((group * pitch + 7, LANES), F32),
                pltpu.VMEM((n * PAIRS * group, LANES), F32),
                pltpu.VMEM((n, PAIRS * group, LANES), F32),
                pltpu.VMEM((PLANES, ROWS, COLS), F32),
                pltpu.SemaphoreType.DMA((3,)),
                pltpu.SemaphoreType.DMA((2, 2)),
                pltpu.SemaphoreType.DMA((2, 2)),
                pltpu.SemaphoreType.DMA((2, 2)),
                pltpu.SemaphoreType.DMA((2, 2)),
                pltpu.SemaphoreType.DMA((n,)),
                pltpu.SemaphoreType.DMA((n,)),
                pltpu.SemaphoreType.DMA((n,)),
                pltpu.SemaphoreType.DMA((n,)),
                pltpu.SemaphoreType.DMA((3,)),
            ],
            compiler_params=pltpu.CompilerParams(
                collective_id=0, has_side_effects=True, vmem_limit_bytes=60 * 1024 * 1024
            ),
        )(observed, estimate, column_weights, plane_taps, row_taps, shear_planes)

    placed = (P("scan", "lat", None), P("scan", "lat", None), P(), P(), P(), P())
    return jax.shard_map(
        on_device, mesh=mesh, in_specs=placed, out_specs=P("scan", "lat", None), check_vma=False
    )
```

time: 234 us -> 141 us (0.60)
  the two profiles are of different devices: /device:TPU:2 before, /device:TPU:31 now
where the time goes in v1:
time: 141 us
  Pallas kernels  138 us (98%)
  local copies, waits for them, and re-layouts  2.67 us (2%)
    pallas_call x1, Pallas kernels, on_device(): pl.pallas_call(functools.partial(kernel, n, nl), out_shape=jax.ShapeDtype...  138 us

profile of v1, /device:TPU:31, one launch (start us, length us, event | category | flops | bytes accessed | tf_op | source)
XLA Modules:
  0.0 140.5 jit_solution(3042650183554524836)
XLA Ops:
  0.0 137.8 %shard_map.64 = f32[12,64,512]{2,1,0:T(8,128)} custom-call(bf16[12,64,512]{2,1,0:T(8,128)(2,1)} %obs_h.1, f32[12,64,512]{2,1,0:T(8,128)} %est_h.1, f32[512,512]{1,0:T(8,128)} %w_h.1, f32[7]{0:T(128)} %pt.1, f32[7]{0:T(128)} %rt.1, s32[512]{0:T(512)} %sh.1), custom_call_target="tpu_custom_call" | custom-call | tf_op jit(solution)/shard_map/pallas_call | solution.py:493
  137.8 2.7 %copy.8 = f32[12,64,512]{2,1,0:T(8,128)} copy(f32[12,64,512]{2,1,0:T(8,128)} %shard_map.64) | data formatting | bytes 3145728

commit v2 on v1

v2 whole, which is shorter than its diff:
```python
import functools

import jax
import jax.numpy as jnp
from jax import lax
from jax.experimental import pallas as pl
from jax.experimental.pallas import tpu as pltpu
from jax.sharding import PartitionSpec as P

MESH = pl.DeviceIdType.MESH
F32 = jnp.float32
BF16 = jnp.bfloat16
PLANES = 12
PAIRS = 6
ROWS = 64
COLS = 512
LANES = 128
TILES = COLS // LANES
PAD = 8
HALF = COLS // 2
EDGES = (((0, 320), (320, 512)), ((0, 272), (272, 512)))
RIMS = (((0, 304), (304, 512)), ((0, 288), (288, 512)))
MIXED = (
    (((0, 128), (128, 256), (256, 304)), ((304, 384), (384, 512))),
    (((0, 128), (128, 256)), ((256, 384), (384, 512))),
)


def split(x):
    hi = x.astype(BF16)
    return hi, (x - hi.astype(F32)).astype(BF16)


def dot(a, b):
    return jnp.dot(a, b, preferred_element_type=F32)


def lane_ids(rows):
    return lax.broadcasted_iota(jnp.int32, (rows, LANES), 1)


def half_roll(x):
    return pltpu.roll(x, ROWS, 1)


def row_matrix(taps, flip):
    line = lax.broadcasted_iota(jnp.int32, (LANES, LANES), 0)
    column = lax.broadcasted_iota(jnp.int32, (LANES, LANES), 1)
    same = (line >= ROWS) == (column >= ROWS)
    row = line & (ROWS - 1)
    target = column & (ROWS - 1)
    far = jnp.where(row < ROWS // 2, row + ROWS, row - ROWS)
    own = jnp.zeros((LANES, LANES), F32)
    edge = jnp.zeros((LANES, LANES), F32)
    for b in range(-3, 4):
        tap = taps[3 - b] if flip else taps[b + 3]
        own = jnp.where(same & (row - target == b), tap, own)
        edge = jnp.where(same & (far - target == b), tap, edge)
    return jnp.concatenate([own, edge], axis=0)


def kernel(
    n,
    nl,
    obs_h,
    est_h,
    w_h,
    pt,
    rt,
    sh,
    out_h,
    obs,
    est,
    w,
    est_t,
    obs_t,
    wmat,
    tmat,
    edge_s,
    edge_r,
    rim_s,
    rim_r,
    hc,
    zf,
    zq,
    bp,
    rhi,
    rlo,
    upd,
    got,
    lined,
    back,
    fin,
    outv,
    in_sem,
    edge_ss,
    edge_rs,
    rim_ss,
    rim_rs,
    a_ss,
    a_rs,
    b_ss,
    b_rs,
    own_sem,
):
    group = HALF // n
    pitch = 2 * PLANES * n + 9
    me = lax.axis_index("scan")
    lat = lax.axis_index("lat")
    s_prev, s_next = lax.rem(me + n - 1, n), lax.rem(me + 1, n)
    l_prev, l_next = lax.rem(lat + nl - 1, nl), lax.rem(lat + 1, nl)

    barrier = pltpu.get_barrier_semaphore()

    def greet(k, carry):
        pl.semaphore_signal(barrier, inc=1, device_id={"scan": lax.rem(me + k, n), "lat": lat}, device_id_type=MESH)
        return carry

    for other in (l_prev, l_next):
        pl.semaphore_signal(barrier, inc=1, device_id={"scan": me, "lat": other}, device_id_type=MESH)
    lax.fori_loop(1, n, greet, 0)

    loads = [
        pltpu.make_async_copy(est_h, est, in_sem.at[0]),
        pltpu.make_async_copy(w_h, w, in_sem.at[1]),
        pltpu.make_async_copy(obs_h, obs, in_sem.at[2]),
    ]
    for load in loads:
        load.start()

    def rows_of(lo, hi, body):
        count = (hi - lo) // 64

        def one(i, carry):
            body(pl.multiple_of(lo + i * 64, 8), 64)
            return carry

        if count:
            lax.fori_loop(0, count, one, 0)
        if lo + 64 * count < hi:
            body(lo + 64 * count, hi - lo - 64 * count)

    def send_edges(stage, part, field):
        lo, hi = EDGES[stage][part]

        def chunk(r, size):
            at = pl.ds(r, size)
            lane = lane_ids(size)
            packed = jnp.zeros((size, LANES), F32)
            for m in range(PAIRS):
                x = field[m, at, :]
                moved = pltpu.roll(x, 6 * m, 1) if m else x
                window = (lane + (3 + ROWS - 6 * m)) & (ROWS - 1)
                packed = jnp.where(window < 6, moved, packed)
            edge_s[stage, at, :] = packed

        rows_of(lo, hi, chunk)
        copies = [
            pltpu.make_async_remote_copy(
                src_ref=edge_s.at[stage, lo:hi],
                dst_ref=edge_r.at[stage, i, lo:hi],
                send_sem=edge_ss.at[stage, part, i],
                recv_sem=edge_rs.at[stage, part, i],
                device_id={"scan": me, "lat": other},
                device_id_type=MESH,
            )
            for i, other in ((0, l_next), (1, l_prev))
        ]
        return copies

    def join_edges(stage, part, copies):
        for copy in copies:
            copy.wait_recv()

        def chunk(r, size):
            at = pl.ds(r, size)
            spot = (lane_ids(size) + 3) & (ROWS - 1)
            first = lax.rem(spot, 6) < 3
            before = jnp.where(lat > 0, edge_r[stage, 0, at, :], 0.0)
            after = jnp.where(lat < nl - 1, edge_r[stage, 1, at, :], 0.0)
            hc[at, :] = jnp.where(first, before, after)

        rows_of(*EDGES[stage][part], chunk)

    def row_pass(stage, part, field):
        lo, hi = EDGES[stage][part]
        middle = (lo + hi) // 32 * 16
        for r0, r1 in ((lo, middle), (middle, hi)):
            edges = hc[r0:r1, :]
            for m in range(PAIRS):
                moved = pltpu.roll(edges, LANES - 6 * m, 1) if m else edges
                hi_x, lo_x = split(jnp.concatenate([field[m, r0:r1, :], moved], axis=1))
                t_hi, t_lo = tmat[stage, 0], tmat[stage, 1]
                y_hi, y_lo = split(dot(hi_x, t_hi) + dot(lo_x, t_hi) + dot(hi_x, t_lo))
                rhi[r0:r1, m * LANES : (m + 1) * LANES] = y_hi
                rlo[r0:r1, m * LANES : (m + 1) * LANES] = y_lo

    def mix(stage, blocks, store):
        for r0, r1 in blocks:
            k0, k1 = max(0, r0 - 8) // LANES * LANES, min(COLS, -(-(r1 + 8) // LANES) * LANES)
            w_hi, w_lo = wmat[stage, 0, r0:r1, k0:k1], wmat[stage, 1, r0:r1, k0:k1]
            for pair in range(PAIRS // 2):
                lanes = slice(pair * 2 * LANES, (pair + 1) * 2 * LANES)
                x_hi, x_lo = rhi[k0:k1, lanes], rlo[k0:k1, lanes]
                y = dot(w_hi, x_hi) + dot(w_hi, x_lo) + dot(w_lo, x_hi)
                store(2 * pair, r0, r1, y[:, :LANES])
                store(2 * pair + 1, r0, r1, y[:, LANES:])

    def send_rims(stage, part, zf):
        lo, hi = RIMS[stage][part]
        length = hi - lo
        base = 3 * lo // 2

        def chunk(r, size):
            low = lane_ids(size) < ROWS
            at, to = pl.ds(r + PAD, size), pl.ds(r + (base - lo), size)
            rim_s[stage, 0, to, :] = jnp.where(low, half_roll(zf[6, at, :]), zf[7, at, :])
            rim_s[stage, 1, to, :] = jnp.where(low, zf[3, at, :], half_roll(zf[4, at, :]))

        rows_of(lo, hi, chunk)

        def rest(r, size):
            low = lane_ids(size) < ROWS
            at, far, to = pl.ds(r + PAD, size), pl.ds(r + PAD + length // 2, size), pl.ds(r + (base - lo + length), size)
            rim_s[stage, 0, to, :] = jnp.where(low, half_roll(zf[8, at, :]), zf[8, far, :])
            rim_s[stage, 1, to, :] = jnp.where(low, zf[5, at, :], half_roll(zf[5, far, :]))

        rows_of(lo, lo + length // 2, rest)
        span = slice(base, base + 3 * length // 2)
        copies = [
            pltpu.make_async_remote_copy(
                src_ref=rim_s.at[stage, i, span],
                dst_ref=rim_r.at[stage, i, span],
                send_sem=rim_ss.at[stage, part, i],
                recv_sem=rim_rs.at[stage, part, i],
                device_id={"scan": other, "lat": lat},
                device_id_type=MESH,
            )
            for i, other in ((0, s_next), (1, s_prev))
        ]
        for copy in copies:
            copy.start()
        return copies

    def join_rims(stage, part, copies, zf):
        lo, hi = RIMS[stage][part]
        length = hi - lo
        base = 3 * lo // 2
        for copy in copies:
            copy.wait_recv()

        def chunk(r, size):
            low = lane_ids(size) < ROWS
            at, to = pl.ds(r + PAD, size), pl.ds(r + (base - lo), size)
            before = jnp.where(me > 0, rim_r[stage, 0, to, :], 0.0)
            after = jnp.where(me < n - 1, rim_r[stage, 1, to, :], 0.0)
            zf[0, at, :] = jnp.where(low, before, half_roll(zf[6, at, :]))
            zf[1, at, :] = half_roll(jnp.where(low, zf[7, at, :], before))
            zf[9, at, :] = half_roll(jnp.where(low, after, zf[3, at, :]))
            zf[10, at, :] = jnp.where(low, half_roll(zf[4, at, :]), after)

        rows_of(lo, hi, chunk)

        def rest(r, size):
            low = lane_ids(size) < ROWS
            at, far, to = pl.ds(r + PAD, size), pl.ds(r + PAD + length // 2, size), pl.ds(r + (base - lo + length), size)
            before = jnp.where(me > 0, rim_r[stage, 0, to, :], 0.0)
            after = jnp.where(me < n - 1, rim_r[stage, 1, to, :], 0.0)
            zf[2, at, :] = jnp.where(low, before, half_roll(zf[8, at, :]))
            zf[2, far, :] = half_roll(jnp.where(low, zf[8, far, :], before))
            zf[11, at, :] = half_roll(jnp.where(low, after, zf[5, at, :]))
            zf[11, far, :] = jnp.where(low, half_roll(zf[5, far, :]), after)

        rows_of(lo, lo + length // 2, rest)

    def plane_pass(flip, lo, hi, zf, store):
        taps = [pt[3 - a] if flip else pt[a + 3] for a in range(-3, 4)]

        def chunk(r, size):
            for m in range(PAIRS):
                total = None
                for a in range(-3, 4):
                    term = taps[a + 3] * zf[m + 3 + a, pl.ds(r + (PAD - 2 * a), size), :]
                    total = term if total is None else total + term
                store(m, pl.ds(r, size), total)

        rows_of(lo, hi, chunk)

    for m in range(2 * PAIRS):
        for field in (zf, zq):
            field[m, 0:PAD, :] = jnp.zeros((PAD, LANES), F32)
            field[m, PAD + COLS : PAD + COLS + PAD, :] = jnp.zeros((PAD, LANES), F32)

    def clear(i, carry):
        for c in range(2 * group):
            lined[pl.ds(c * pitch + 8 * i, 8), :] = jnp.zeros((8, LANES), F32)
        return carry

    loads[0].wait()

    def turn(source, target):
        def one(m, carry):
            for k in range(TILES):
                lanes = slice(k * LANES, (k + 1) * LANES)
                x = jnp.concatenate([source[m, :, lanes], source[m + PAIRS, :, lanes]], axis=0)
                target[m, lanes, :] = x.astype(F32).T
            return carry

        lax.fori_loop(0, PAIRS, one, 0)

    turn(est, est_t)
    edges = [send_edges(0, part, est_t) for part in range(2)]
    pl.semaphore_wait(barrier, n + 1)
    for copies in edges:
        for copy in copies:
            copy.start()
    sent = edges[0] + edges[1]

    for stage in range(2):
        hi, lo = split(row_matrix(rt, stage == 1))
        tmat[stage, 0] = hi
        tmat[stage, 1] = lo
    rhi[EDGES[0][0][1] : 3 * LANES, :] = jnp.zeros((3 * LANES - EDGES[0][0][1], PAIRS * LANES), BF16)
    rlo[EDGES[0][0][1] : 3 * LANES, :] = jnp.zeros((3 * LANES - EDGES[0][0][1], PAIRS * LANES), BF16)
    loads[1].wait()
    for i in range(TILES):
        for j in range(TILES):
            x = w[i * LANES : (i + 1) * LANES, j * LANES : (j + 1) * LANES]
            hi, lo = split(x)
            wmat[1, 0, i * LANES : (i + 1) * LANES, j * LANES : (j + 1) * LANES] = hi
            wmat[1, 1, i * LANES : (i + 1) * LANES, j * LANES : (j + 1) * LANES] = lo
            hi, lo = split(x.T)
            wmat[0, 0, j * LANES : (j + 1) * LANES, i * LANES : (i + 1) * LANES] = hi
            wmat[0, 1, j * LANES : (j + 1) * LANES, i * LANES : (i + 1) * LANES] = lo

    def to_field(m, r0, r1, y):
        zf[m + 3, PAD + r0 : PAD + r1, :] = y

    rims = []
    for part in range(2):
        join_edges(0, part, edges[part])
        row_pass(0, part, est_t)
        mix(0, MIXED[0][part], to_field)
        rims.append(send_rims(0, part, zf))
    sent += rims[0] + rims[1]
    loads[2].wait()
    turn(obs, obs_t)
    lax.fori_loop(0, PLANES * n // 8, clear, 0)

    def to_quotient(m, at, total):
        bp[m, at, :] = obs_t[m, at, :] / total

    def place(r, size):
        for m in range(PAIRS):
            zq[m + 3, pl.ds(r + PAD, size), :] = bp[m, pl.ds(r, size), :]

    backs = []
    for part in range(2):
        join_rims(0, part, rims[part], zf)
        plane_pass(False, *RIMS[1][part], zf, to_quotient)
        rows_of(*RIMS[1][part], place)
        backs.append(send_rims(1, part, zq))
    sent += backs[0] + backs[1]

    def to_back(m, at, total):
        bp[m, at, :] = total

    edges = []
    for part in range(2):
        join_rims(1, part, backs[part], zq)
        plane_pass(True, *EDGES[1][part], zq, to_back)
        edges.append(send_edges(1, part, bp))
        for copy in edges[part]:
            copy.start()
    sent += edges[0] + edges[1]

    def to_updated(m, r0, r1, y):
        upd[m, r0:r1, :] = est_t[m, r0:r1, :] * y

    def first_copy(part, k):
        dest = lax.rem(me + k, n)
        return pltpu.make_async_remote_copy(
            src_ref=upd.at[:, pl.ds(pl.multiple_of(part * HALF + dest * group, 8), group), :],
            dst_ref=got.at[part, me],
            send_sem=a_ss.at[part, k],
            recv_sem=a_rs.at[part, me],
            device_id={"scan": dest, "lat": lat},
            device_id_type=MESH,
        )

    def second_copy(part, k):
        dest = lax.rem(me + k, n)
        return pltpu.make_async_remote_copy(
            src_ref=back.at[part, pl.ds(pl.multiple_of(dest * PAIRS * group, 8), PAIRS * group), :],
            dst_ref=fin.at[part, me],
            send_sem=b_ss.at[part, k],
            recv_sem=b_rs.at[part, me],
            device_id={"scan": dest, "lat": lat},
            device_id_type=MESH,
        )

    for part in range(2):
        join_edges(1, part, edges[part])
        row_pass(1, part, bp)
        mix(1, MIXED[1][part], to_updated)

        def start_first(k, carry):
            first_copy(part, k).start()
            return carry

        lax.fori_loop(1, n, start_first, 0)
        mine = pltpu.make_async_copy(
            upd.at[:, pl.ds(pl.multiple_of(part * HALF + me * group, 8), group), :], got.at[part, me], own_sem.at[part]
        )
        mine.start()

    for part in range(2):
        pltpu.make_async_copy(upd.at[:, 0:group, :], got.at[part, me], own_sem.at[part]).wait()

        def line_up(s):
            low = lane_ids(8) < ROWS
            for m in range(PAIRS):
                x = got[part, s, m]
                y = half_roll(x)
                start = part * group * pitch + PLANES * n + PLANES * s + m
                lined[pl.ds(start, group, stride=pitch), :] = jnp.where(low, x, y)
                lined[pl.ds(start + PAIRS, group, stride=pitch), :] = jnp.where(low, y, x)

        line_up(me)

        def take_first(k, carry):
            s = lax.rem(me - k + n, n)
            pltpu.make_async_remote_copy(
                src_ref=upd.at[:, pl.ds(0, group), :],
                dst_ref=got.at[part, s],
                send_sem=a_ss.at[part, k],
                recv_sem=a_rs.at[part, s],
                device_id={"scan": s, "lat": lat},
                device_id_type=MESH,
            ).wait_recv()
            line_up(s)
            return carry

        lax.fori_loop(1, n, take_first, 0)

        def shear(dest):
            low = lane_ids(8) < ROWS
            for c in range(group):
                at = (part * group + c) * pitch + PLANES * n + PLANES * dest - sh[part * HALF + me * group + c]
                x = jnp.where(low, lined[pl.ds(at, 8), :], lined[pl.ds(at + PAIRS, 8), :])
                back[part, pl.ds(dest * (PAIRS * group) + c, PAIRS, stride=group), :] = x[:PAIRS]

        def start_second(k, carry):
            shear(lax.rem(me + k, n))
            second_copy(part, k).start()
            return carry

        lax.fori_loop(1, n, start_second, 0)
        shear(me)
        mine = pltpu.make_async_copy(
            back.at[part, pl.ds(pl.multiple_of(me * PAIRS * group, 8), PAIRS * group), :],
            fin.at[part, me],
            own_sem.at[2 + part],
        )
        mine.start()

    per = LANES // group
    for part in range(2):
        pltpu.make_async_copy(back.at[part, pl.ds(0, PAIRS * group), :], fin.at[part, me], own_sem.at[2 + part]).wait()

        def take_second(k, carry):
            s = lax.rem(me - k + n, n)
            pltpu.make_async_remote_copy(
                src_ref=back.at[part, pl.ds(0, PAIRS * group), :],
                dst_ref=fin.at[part, s],
                send_sem=b_ss.at[part, k],
                recv_sem=b_rs.at[part, s],
                device_id={"scan": s, "lat": lat},
                device_id_type=MESH,
            ).wait_recv()
            return carry

        lax.fori_loop(1, n, take_second, 0)
        for k in range(TILES // 2):
            lanes = slice(part * HALF + k * LANES, part * HALF + (k + 1) * LANES)
            for m in range(PAIRS):
                x = jnp.concatenate(
                    [fin[part, k * per + j, m * group : (m + 1) * group, :] for j in range(per)], axis=0
                ).T
                outv[m, :, lanes] = x[:ROWS]
                outv[m + PAIRS, :, lanes] = x[ROWS:]
        half = slice(part * HALF, (part + 1) * HALF)
        pltpu.make_async_copy(outv.at[:, :, half], out_h.at[:, :, half], own_sem.at[4 + part]).start()

    for copy in sent:
        copy.wait_send()

    def drain(k, carry):
        for part in range(2):
            first_copy(part, k).wait_send()
            second_copy(part, k).wait_send()
        return carry

    lax.fori_loop(1, n, drain, 0)
    for part in range(2):
        half = slice(part * HALF, (part + 1) * HALF)
        pltpu.make_async_copy(outv.at[:, :, half], out_h.at[:, :, half], own_sem.at[4 + part]).wait()

def solution(mesh):
    n, nl = mesh.shape["scan"], mesh.shape["lat"]
    group = HALF // n
    pitch = 2 * PLANES * n + 9

    def on_device(observed, estimate, column_weights, plane_taps, row_taps, shear_planes):
        any_space = pl.BlockSpec(memory_space=pl.ANY)
        scalars = pl.BlockSpec(memory_space=pltpu.SMEM)
        return pl.pallas_call(
            functools.partial(kernel, n, nl),
            out_shape=jax.ShapeDtypeStruct((PLANES, ROWS, COLS), F32),
            in_specs=[any_space, any_space, any_space, scalars, scalars, scalars],
            out_specs=any_space,
            scratch_shapes=[
                pltpu.VMEM((PLANES, ROWS, COLS), BF16),
                pltpu.VMEM((PLANES, ROWS, COLS), F32),
                pltpu.VMEM((COLS, COLS), F32),
                pltpu.VMEM((PAIRS, COLS, LANES), F32),
                pltpu.VMEM((PAIRS, COLS, LANES), F32),
                pltpu.VMEM((2, 2, COLS, COLS), BF16),
                pltpu.VMEM((2, 2, 2 * LANES, LANES), BF16),
                pltpu.VMEM((2, COLS, LANES), F32),
                pltpu.VMEM((2, 2, COLS, LANES), F32),
                pltpu.VMEM((2, 2, 3 * COLS // 2, LANES), F32),
                pltpu.VMEM((2, 2, 3 * COLS // 2, LANES), F32),
                pltpu.VMEM((COLS, LANES), F32),
                pltpu.VMEM((2 * PAIRS, COLS + 2 * PAD, LANES), F32),
                pltpu.VMEM((2 * PAIRS, COLS + 2 * PAD, LANES), F32),
                pltpu.VMEM((PAIRS, COLS, LANES), F32),
                pltpu.VMEM((COLS, PAIRS * LANES), BF16),
                pltpu.VMEM((COLS, PAIRS * LANES), BF16),
                pltpu.VMEM((PAIRS, COLS, LANES), F32),
                pltpu.VMEM((2, n, PAIRS, group, LANES), F32),
                pltpu.VMEM((2 * group * pitch + 7, LANES), F32),
                pltpu.VMEM((2, n * PAIRS * group, LANES), F32),
                pltpu.VMEM((2, n, PAIRS * group, LANES), F32),
                pltpu.VMEM((PLANES, ROWS, COLS), F32),
                pltpu.SemaphoreType.DMA((3,)),
                pltpu.SemaphoreType.DMA((2, 2, 2)),
                pltpu.SemaphoreType.DMA((2, 2, 2)),
                pltpu.SemaphoreType.DMA((2, 2, 2)),
                pltpu.SemaphoreType.DMA((2, 2, 2)),
                pltpu.SemaphoreType.DMA((2, n)),
                pltpu.SemaphoreType.DMA((2, n)),
                pltpu.SemaphoreType.DMA((2, n)),
                pltpu.SemaphoreType.DMA((2, n)),
                pltpu.SemaphoreType.DMA((6,)),
            ],
            compiler_params=pltpu.CompilerParams(
                collective_id=0, has_side_effects=True, vmem_limit_bytes=60 * 1024 * 1024
            ),
        )(observed, estimate, column_weights, plane_taps, row_taps, shear_planes)

    placed = (P("scan", "lat", None), P("scan", "lat", None), P(), P(), P(), P())
    return jax.shard_map(
        on_device, mesh=mesh, in_specs=placed, out_specs=P("scan", "lat", None), check_vma=False
    )
```

time: 141 us -> 120 us (0.85)
  Pallas kernels: 138 us -> 117 us
    pallas_call x1, Pallas kernels: 138 us -> 117 us  [on_device(): pl.pallas_call(functools.partial(kernel, n, nl), out_shape=jax.ShapeDtype...]
where the time goes in v2:
time: 120 us; the launch traced here: 119 us
  Pallas kernels  117 us (98%)
  local copies, waits for them, and re-layouts  2.67 us (2%)
    pallas_call x1, Pallas kernels, on_device(): pl.pallas_call(functools.partial(kernel, n, nl), out_shape=jax.ShapeDtype...  117 us
    unnamed x1, local copies, waits for them, and re-layouts  2.67 us

profile of v2, /device:TPU:31, one launch (start us, length us, event | category | flops | bytes accessed | tf_op | source)
XLA Modules:
  0.0 119.5 jit_solution(9776193688585799083)
XLA Ops:
  0.0 116.8 %shard_map.64 = f32[12,64,512]{2,1,0:T(8,128)} custom-call(bf16[12,64,512]{2,1,0:T(8,128)(2,1)} %obs_h.1, f32[12,64,512]{2,1,0:T(8,128)} %est_h.1, f32[512,512]{1,0:T(8,128)} %w_h.1, f32[7]{0:T(128)} %pt.1, f32[7]{0:T(128)} %rt.1, s32[512]{0:T(512)} %sh.1), custom_call_target="tpu_custom_call" | custom-call | tf_op jit(solution)/shard_map/pallas_call | solution.py:517
  116.8 2.7 %copy.8 = f32[12,64,512]{2,1,0:T(8,128)} copy(f32[12,64,512]{2,1,0:T(8,128)} %shard_map.64) | data formatting | bytes 3145728

commit v3 on v2

--- a/solution.py
+++ b/solution.py
@@ -18,12 +18,17 @@
 TILES = COLS // LANES
 PAD = 8
 HALF = COLS // 2
-EDGES = (((0, 320), (320, 512)), ((0, 272), (272, 512)))
-RIMS = (((0, 304), (304, 512)), ((0, 288), (288, 512)))
-MIXED = (
-    (((0, 128), (128, 256), (256, 304)), ((304, 384), (384, 512))),
-    (((0, 128), (128, 256)), ((256, 384), (384, 512))),
-)
+PARTS = 4
+
+
+def ranges(margin):
+    ends = [min(COLS, LANES * (part + 1) + margin) for part in range(PARTS - 1)] + [COLS]
+    return tuple(zip([0] + ends[:-1], ends))
+
+
+EDGES = (ranges(64), ranges(16))
+RIMS = (ranges(48), ranges(32))
+MIXED = (RIMS[0], ranges(0))
 
 
 def split(x):
@@ -102,8 +107,10 @@
     b_ss,
     b_rs,
     own_sem,
+    far,
 ):
     group = HALF // n
+    share = group // 2
     pitch = 2 * PLANES * n + 9
     me = lax.axis_index("scan")
     lat = lax.axis_index("lat")
@@ -112,13 +119,20 @@
 
     barrier = pltpu.get_barrier_semaphore()
 
-    def greet(k, carry):
-        pl.semaphore_signal(barrier, inc=1, device_id={"scan": lax.rem(me + k, n), "lat": lat}, device_id_type=MESH)
-        return carry
-
+    def greet(sem, other):
+        pl.semaphore_signal(sem, inc=1, device_id=other, device_id_type=MESH)
+
+    for other in (s_prev, s_next):
+        greet(barrier, {"scan": other, "lat": lat})
     for other in (l_prev, l_next):
-        pl.semaphore_signal(barrier, inc=1, device_id={"scan": me, "lat": other}, device_id_type=MESH)
-    lax.fori_loop(1, n, greet, 0)
+        greet(barrier, {"scan": me, "lat": other})
+
+    def spread(i, reach):
+        for other in (lax.rem(me + n - reach, n), lax.rem(me + reach, n)):
+            greet(far.at[i], {"scan": other, "lat": lat})
+
+    def gather(i):
+        pl.semaphore_wait(far.at[i], 2)
 
     loads = [
         pltpu.make_async_copy(est_h, est, in_sem.at[0]),
@@ -190,21 +204,21 @@
             for m in range(PAIRS):
                 moved = pltpu.roll(edges, LANES - 6 * m, 1) if m else edges
                 hi_x, lo_x = split(jnp.concatenate([field[m, r0:r1, :], moved], axis=1))
-                t_hi, t_lo = tmat[stage, 0], tmat[stage, 1]
-                y_hi, y_lo = split(dot(hi_x, t_hi) + dot(lo_x, t_hi) + dot(hi_x, t_lo))
+                both = dot(hi_x, tmat[stage, 0])
+                y_hi, y_lo = split(both[:, :LANES] + both[:, LANES:] + dot(lo_x, tmat[stage, 0, :, :LANES]))
                 rhi[r0:r1, m * LANES : (m + 1) * LANES] = y_hi
                 rlo[r0:r1, m * LANES : (m + 1) * LANES] = y_lo
 
-    def mix(stage, blocks, store):
-        for r0, r1 in blocks:
-            k0, k1 = max(0, r0 - 8) // LANES * LANES, min(COLS, -(-(r1 + 8) // LANES) * LANES)
-            w_hi, w_lo = wmat[stage, 0, r0:r1, k0:k1], wmat[stage, 1, r0:r1, k0:k1]
-            for pair in range(PAIRS // 2):
-                lanes = slice(pair * 2 * LANES, (pair + 1) * 2 * LANES)
-                x_hi, x_lo = rhi[k0:k1, lanes], rlo[k0:k1, lanes]
-                y = dot(w_hi, x_hi) + dot(w_hi, x_lo) + dot(w_lo, x_hi)
-                store(2 * pair, r0, r1, y[:, :LANES])
-                store(2 * pair + 1, r0, r1, y[:, LANES:])
+    def mix(stage, part, store):
+        r0, r1 = MIXED[stage][part]
+        k0, k1 = max(0, r0 - 8) // LANES * LANES, min(COLS, -(-(r1 + 8) // LANES) * LANES)
+        w_hi, w_lo = wmat[stage, 0, r0:r1, k0:k1], wmat[stage, 1, r0:r1, k0:k1]
+        for pair in range(PAIRS // 2):
+            lanes = slice(pair * 2 * LANES, (pair + 1) * 2 * LANES)
+            x_hi, x_lo = rhi[k0:k1, lanes], rlo[k0:k1, lanes]
+            y = dot(w_hi, x_hi) + dot(w_hi, x_lo) + dot(w_lo, x_hi)
+            store(2 * pair, r0, r1, y[:, :LANES])
+            store(2 * pair + 1, r0, r1, y[:, LANES:])
 
     def send_rims(stage, part, zf):
         lo, hi = RIMS[stage][part]
@@ -298,9 +312,9 @@
 
     loads[0].wait()
 
-    def turn(source, target):
+    def turn(source, target, tiles):
         def one(m, carry):
-            for k in range(TILES):
+            for k in tiles:
                 lanes = slice(k * LANES, (k + 1) * LANES)
                 x = jnp.concatenate([source[m, :, lanes], source[m + PAIRS, :, lanes]], axis=0)
                 target[m, lanes, :] = x.astype(F32).T
@@ -308,44 +322,42 @@
 
         lax.fori_loop(0, PAIRS, one, 0)
 
-    turn(est, est_t)
-    edges = [send_edges(0, part, est_t) for part in range(2)]
-    pl.semaphore_wait(barrier, n + 1)
-    for copies in edges:
-        for copy in copies:
+    sent = []
+    first_edges = {}
+
+    def open_edges(part):
+        first_edges[part] = send_edges(0, part, est_t)
+        if part == 0:
+            pl.semaphore_wait(barrier, 4)
+        for copy in first_edges[part]:
             copy.start()
-    sent = edges[0] + edges[1]
-
-    for stage in range(2):
+        sent.extend(first_edges[part])
+
+    def weights(stage):
+        for i in range(TILES):
+            for j in range(max(0, i - 1), min(TILES, i + 2)):
+                rows, columns = slice(i * LANES, (i + 1) * LANES), slice(j * LANES, (j + 1) * LANES)
+                hi, lo = split(w[rows, columns] if stage else w[columns, rows].T)
+                wmat[stage, 0, rows, columns] = hi
+                wmat[stage, 1, rows, columns] = lo
         hi, lo = split(row_matrix(rt, stage == 1))
-        tmat[stage, 0] = hi
-        tmat[stage, 1] = lo
-    rhi[EDGES[0][0][1] : 3 * LANES, :] = jnp.zeros((3 * LANES - EDGES[0][0][1], PAIRS * LANES), BF16)
-    rlo[EDGES[0][0][1] : 3 * LANES, :] = jnp.zeros((3 * LANES - EDGES[0][0][1], PAIRS * LANES), BF16)
+        tmat[stage, 0, :, :LANES] = hi
+        tmat[stage, 0, :, LANES:] = lo
+
+    turn(est, est_t, (0, 1))
+    open_edges(0)
+    turn(est, est_t, (2, 3))
+    for part in range(1, PARTS):
+        open_edges(part)
+    spread(0, 1)
     loads[1].wait()
-    for i in range(TILES):
-        for j in range(TILES):
-            x = w[i * LANES : (i + 1) * LANES, j * LANES : (j + 1) * LANES]
-            hi, lo = split(x)
-            wmat[1, 0, i * LANES : (i + 1) * LANES, j * LANES : (j + 1) * LANES] = hi
-            wmat[1, 1, i * LANES : (i + 1) * LANES, j * LANES : (j + 1) * LANES] = lo
-            hi, lo = split(x.T)
-            wmat[0, 0, j * LANES : (j + 1) * LANES, i * LANES : (i + 1) * LANES] = hi
-            wmat[0, 1, j * LANES : (j + 1) * LANES, i * LANES : (i + 1) * LANES] = lo
+    weights(0)
+    rest_rows = slice(EDGES[0][0][1], COLS)
+    rhi[rest_rows, :] = jnp.zeros((COLS - EDGES[0][0][1], PAIRS * LANES), BF16)
+    rlo[rest_rows, :] = jnp.zeros((COLS - EDGES[0][0][1], PAIRS * LANES), BF16)
 
     def to_field(m, r0, r1, y):
         zf[m + 3, PAD + r0 : PAD + r1, :] = y
-
-    rims = []
-    for part in range(2):
-        join_edges(0, part, edges[part])
-        row_pass(0, part, est_t)
-        mix(0, MIXED[0][part], to_field)
-        rims.append(send_rims(0, part, zf))
-    sent += rims[0] + rims[1]
-    loads[2].wait()
-    turn(obs, obs_t)
-    lax.fori_loop(0, PLANES * n // 8, clear, 0)
 
     def to_quotient(m, at, total):
         bp[m, at, :] = obs_t[m, at, :] / total
@@ -354,42 +366,35 @@
         for m in range(PAIRS):
             zq[m + 3, pl.ds(r + PAD, size), :] = bp[m, pl.ds(r, size), :]
 
-    backs = []
-    for part in range(2):
-        join_rims(0, part, rims[part], zf)
-        plane_pass(False, *RIMS[1][part], zf, to_quotient)
-        rows_of(*RIMS[1][part], place)
-        backs.append(send_rims(1, part, zq))
-    sent += backs[0] + backs[1]
-
     def to_back(m, at, total):
         bp[m, at, :] = total
 
-    edges = []
-    for part in range(2):
-        join_rims(1, part, backs[part], zq)
-        plane_pass(True, *EDGES[1][part], zq, to_back)
-        edges.append(send_edges(1, part, bp))
-        for copy in edges[part]:
-            copy.start()
-    sent += edges[0] + edges[1]
-
     def to_updated(m, r0, r1, y):
         upd[m, r0:r1, :] = est_t[m, r0:r1, :] * y
 
+    def order(k):
+        return jnp.where(k == n - 1, k, lax.rem(4 * k, n - 1))
+
     def first_copy(part, k):
-        dest = lax.rem(me + k, n)
+        dest = lax.rem(me + order(k), n)
         return pltpu.make_async_remote_copy(
-            src_ref=upd.at[:, pl.ds(pl.multiple_of(part * HALF + dest * group, 8), group), :],
-            dst_ref=got.at[part, me],
+            src_ref=upd.at[:, pl.ds(pl.multiple_of(part * LANES + dest * share, share), share), :],
+            dst_ref=got.at[part // 2, me, :, share * (part % 2) : share * (part % 2 + 1), :],
             send_sem=a_ss.at[part, k],
             recv_sem=a_rs.at[part, me],
             device_id={"scan": dest, "lat": lat},
             device_id_type=MESH,
         )
 
+    def own_first(part):
+        return pltpu.make_async_copy(
+            upd.at[:, pl.ds(pl.multiple_of(part * LANES + me * share, share), share), :],
+            got.at[part // 2, me, :, share * (part % 2) : share * (part % 2 + 1), :],
+            own_sem.at[part],
+        )
+
     def second_copy(part, k):
-        dest = lax.rem(me + k, n)
+        dest = lax.rem(me + order(k), n)
         return pltpu.make_async_remote_copy(
             src_ref=back.at[part, pl.ds(pl.multiple_of(dest * PAIRS * group, 8), PAIRS * group), :],
             dst_ref=fin.at[part, me],
@@ -399,23 +404,79 @@
             device_id_type=MESH,
         )
 
-    for part in range(2):
-        join_edges(1, part, edges[part])
+    rims, backs, last_edges = {}, {}, {}
+
+    def step_field(part):
+        join_edges(0, part, first_edges[part])
+        row_pass(0, part, est_t)
+        mix(0, part, to_field)
+        rims[part] = send_rims(0, part, zf)
+
+    def step_quotient(part):
+        join_rims(0, part, rims[part], zf)
+        plane_pass(False, *RIMS[1][part], zf, to_quotient)
+        rows_of(*RIMS[1][part], place)
+        backs[part] = send_rims(1, part, zq)
+
+    def step_planes(part):
+        join_rims(1, part, backs[part], zq)
+        plane_pass(True, *EDGES[1][part], zq, to_back)
+        last_edges[part] = send_edges(1, part, bp)
+        for copy in last_edges[part]:
+            copy.start()
+
+    def step_update(part):
+        join_edges(1, part, last_edges[part])
         row_pass(1, part, bp)
-        mix(1, MIXED[1][part], to_updated)
+        mix(1, part, to_updated)
 
         def start_first(k, carry):
             first_copy(part, k).start()
             return carry
 
         lax.fori_loop(1, n, start_first, 0)
-        mine = pltpu.make_async_copy(
-            upd.at[:, pl.ds(pl.multiple_of(part * HALF + me * group, 8), group), :], got.at[part, me], own_sem.at[part]
-        )
-        mine.start()
+        own_first(part).start()
+
+    def prepare():
+        loads[2].wait()
+        turn(obs, obs_t, range(TILES))
+
+    def tidy():
+        lax.fori_loop(0, PLANES * n // 8, clear, 0)
+
+    step_field(0)
+    gather(0)
+    spread(1, 2)
+    prepare()
+    step_field(1)
+    step_quotient(0)
+    gather(1)
+    spread(2, 4)
+    step_field(2)
+    weights(1)
+    step_quotient(1)
+    step_planes(0)
+    gather(2)
+    spread(3, 8)
+    step_field(3)
+    gather(3)
+    step_update(0)
+    step_quotient(2)
+    step_planes(1)
+    step_update(1)
+    step_quotient(3)
+    step_planes(2)
+    step_update(2)
+    tidy()
+    step_planes(3)
+    step_update(3)
+    for group_of in (rims, backs, last_edges):
+        for part in range(PARTS):
+            sent += group_of[part]
 
     for part in range(2):
-        pltpu.make_async_copy(upd.at[:, 0:group, :], got.at[part, me], own_sem.at[part]).wait()
+        own_first(2 * part).wait()
+        own_first(2 * part + 1).wait()
 
         def line_up(s):
             low = lane_ids(8) < ROWS
@@ -429,15 +490,16 @@
         line_up(me)
 
         def take_first(k, carry):
-            s = lax.rem(me - k + n, n)
-            pltpu.make_async_remote_copy(
-                src_ref=upd.at[:, pl.ds(0, group), :],
-                dst_ref=got.at[part, s],
-                send_sem=a_ss.at[part, k],
-                recv_sem=a_rs.at[part, s],
-                device_id={"scan": s, "lat": lat},
-                device_id_type=MESH,
-            ).wait_recv()
+            s = lax.rem(me - order(k) + n, n)
+            for i in range(2):
+                pltpu.make_async_remote_copy(
+                    src_ref=upd.at[:, pl.ds(0, share), :],
+                    dst_ref=got.at[part, s, :, share * i : share * (i + 1), :],
+                    send_sem=a_ss.at[2 * part + i, k],
+                    recv_sem=a_rs.at[2 * part + i, s],
+                    device_id={"scan": s, "lat": lat},
+                    device_id_type=MESH,
+                ).wait_recv()
             line_up(s)
             return carry
 
@@ -446,12 +508,12 @@
         def shear(dest):
             low = lane_ids(8) < ROWS
             for c in range(group):
-                at = (part * group + c) * pitch + PLANES * n + PLANES * dest - sh[part * HALF + me * group + c]
+                at = (part * group + c) * pitch + PLANES * n + PLANES * dest - sh[part * HALF + c // share * LANES + me * share + c % share]
                 x = jnp.where(low, lined[pl.ds(at, 8), :], lined[pl.ds(at + PAIRS, 8), :])
                 back[part, pl.ds(dest * (PAIRS * group) + c, PAIRS, stride=group), :] = x[:PAIRS]
 
         def start_second(k, carry):
-            shear(lax.rem(me + k, n))
+            shear(lax.rem(me + order(k), n))
             second_copy(part, k).start()
             return carry
 
@@ -460,16 +522,15 @@
         mine = pltpu.make_async_copy(
             back.at[part, pl.ds(pl.multiple_of(me * PAIRS * group, 8), PAIRS * group), :],
             fin.at[part, me],
-            own_sem.at[2 + part],
+            own_sem.at[4 + part],
         )
         mine.start()
 
-    per = LANES // group
     for part in range(2):
-        pltpu.make_async_copy(back.at[part, pl.ds(0, PAIRS * group), :], fin.at[part, me], own_sem.at[2 + part]).wait()
+        pltpu.make_async_copy(back.at[part, pl.ds(0, PAIRS * group), :], fin.at[part, me], own_sem.at[4 + part]).wait()
 
         def take_second(k, carry):
-            s = lax.rem(me - k + n, n)
+            s = lax.rem(me - order(k) + n, n)
             pltpu.make_async_remote_copy(
                 src_ref=back.at[part, pl.ds(0, PAIRS * group), :],
                 dst_ref=fin.at[part, s],
@@ -481,30 +542,39 @@
             return carry
 
         lax.fori_loop(1, n, take_second, 0)
-        for k in range(TILES // 2):
-            lanes = slice(part * HALF + k * LANES, part * HALF + (k + 1) * LANES)
-            for m in range(PAIRS):
-                x = jnp.concatenate(
-                    [fin[part, k * per + j, m * group : (m + 1) * group, :] for j in range(per)], axis=0
-                ).T
+        first = lax.broadcasted_iota(jnp.int32, (group, LANES), 0) < share
+        for m in range(PAIRS):
+            tiles = ([], [])
+            for j in range(0, n, 2):
+                x = fin[part, j, m * group : (m + 1) * group, :]
+                y = fin[part, j + 1, m * group : (m + 1) * group, :]
+                tiles[0].append(jnp.where(first, x, pltpu.roll(y, share, 0)))
+                tiles[1].append(jnp.where(first, pltpu.roll(x, share, 0), y))
+            for k in range(2):
+                lanes = slice(part * HALF + k * LANES, part * HALF + (k + 1) * LANES)
+                x = jnp.concatenate(tiles[k], axis=0).T
                 outv[m, :, lanes] = x[:ROWS]
                 outv[m + PAIRS, :, lanes] = x[ROWS:]
-        half = slice(part * HALF, (part + 1) * HALF)
-        pltpu.make_async_copy(outv.at[:, :, half], out_h.at[:, :, half], own_sem.at[4 + part]).start()
+            half = slice(part * HALF, (part + 1) * HALF)
+            for plane in (m, m + PAIRS):
+                pltpu.make_async_copy(
+                    outv.at[plane, :, half], out_h.at[plane, :, half], own_sem.at[6 + part]
+                ).start()
 
     for copy in sent:
         copy.wait_send()
 
     def drain(k, carry):
+        for part in range(PARTS):
+            first_copy(part, k).wait_send()
         for part in range(2):
-            first_copy(part, k).wait_send()
             second_copy(part, k).wait_send()
         return carry
 
     lax.fori_loop(1, n, drain, 0)
     for part in range(2):
         half = slice(part * HALF, (part + 1) * HALF)
-        pltpu.make_async_copy(outv.at[:, :, half], out_h.at[:, :, half], own_sem.at[4 + part]).wait()
+        pltpu.make_async_copy(outv.at[:, :, half], out_h.at[:, :, half], own_sem.at[6 + part]).wait()
 
 def solution(mesh):
     n, nl = mesh.shape["scan"], mesh.shape["lat"]
@@ -526,7 +596,7 @@
                 pltpu.VMEM((PAIRS, COLS, LANES), F32),
                 pltpu.VMEM((PAIRS, COLS, LANES), F32),
                 pltpu.VMEM((2, 2, COLS, COLS), BF16),
-                pltpu.VMEM((2, 2, 2 * LANES, LANES), BF16),
+                pltpu.VMEM((2, 1, 2 * LANES, 2 * LANES), BF16),
                 pltpu.VMEM((2, COLS, LANES), F32),
                 pltpu.VMEM((2, 2, COLS, LANES), F32),
                 pltpu.VMEM((2, 2, 3 * COLS // 2, LANES), F32),
@@ -544,15 +614,16 @@
                 pltpu.VMEM((2, n, PAIRS * group, LANES), F32),
                 pltpu.VMEM((PLANES, ROWS, COLS), F32),
                 pltpu.SemaphoreType.DMA((3,)),
-                pltpu.SemaphoreType.DMA((2, 2, 2)),
-                pltpu.SemaphoreType.DMA((2, 2, 2)),
-                pltpu.SemaphoreType.DMA((2, 2, 2)),
-                pltpu.SemaphoreType.DMA((2, 2, 2)),
+                pltpu.SemaphoreType.DMA((2, PARTS, 2)),
+                pltpu.SemaphoreType.DMA((2, PARTS, 2)),
+                pltpu.SemaphoreType.DMA((2, PARTS, 2)),
+                pltpu.SemaphoreType.DMA((2, PARTS, 2)),
+                pltpu.SemaphoreType.DMA((PARTS, n)),
+                pltpu.SemaphoreType.DMA((PARTS, n)),
                 pltpu.SemaphoreType.DMA((2, n)),
                 pltpu.SemaphoreType.DMA((2, n)),
-                pltpu.SemaphoreType.DMA((2, n)),
-                pltpu.SemaphoreType.DMA((2, n)),
-                pltpu.SemaphoreType.DMA((6,)),
+                pltpu.SemaphoreType.DMA((8,)),
+                pltpu.SemaphoreType.REGULAR((4,)),
             ],
             compiler_params=pltpu.CompilerParams(
                 collective_id=0, has_side_effects=True, vmem_limit_bytes=60 * 1024 * 1024

time: 120 us -> 113 us (0.942)
  Pallas kernels: 117 us -> 109 us
    pallas_call x1, Pallas kernels: 117 us -> 109 us  [on_device(): pl.pallas_call(functools.partial(kernel, n, nl), out_shape=jax.ShapeDtype...]
where the time goes in v3:
time: 113 us; the launch traced here: 112 us
  Pallas kernels  109 us (96%)
  local copies, waits for them, and re-layouts  2.67 us (2%)
    pallas_call x1, Pallas kernels, on_device(): pl.pallas_call(functools.partial(kernel, n, nl), out_shape=jax.ShapeDtype...  109 us
    unnamed x1, local copies, waits for them, and re-layouts  2.67 us

profile of v3, /device:TPU:31, one launch (start us, length us, event | category | flops | bytes accessed | tf_op | source)
XLA Modules:
  0.0 112.2 jit_solution(8209001859280186993)
XLA Ops:
  0.0 109.5 %shard_map.64 = f32[12,64,512]{2,1,0:T(8,128)} custom-call(bf16[12,64,512]{2,1,0:T(8,128)(2,1)} %obs_h.1, f32[12,64,512]{2,1,0:T(8,128)} %est_h.1, f32[512,512]{1,0:T(8,128)} %w_h.1, f32[7]{0:T(128)} %pt.1, f32[7]{0:T(128)} %rt.1, s32[512]{0:T(512)} %sh.1), custom_call_target="tpu_custom_call" | custom-call | tf_op jit(solution)/shard_map/pallas_call | solution.py:587
  109.5 2.7 %copy.8 = f32[12,64,512]{2,1,0:T(8,128)} copy(f32[12,64,512]{2,1,0:T(8,128)} %shard_map.64) | data formatting | bytes 3145728
